TPU v7x, 32 devices: a whole 2x2x4 slice. The times are simulated.
32 devices in a mesh: groups: 2 (over y), ctx: 8 (over z, x), head: 2 (over core).
Axes of the slice: x: 2, y: 2, z: 4, core: 2. Of those that a mesh axis runs over, the one named last changes fastest.
Arguments:
- queries: bfloat16 [16, 128, 64, 192], P(('groups', 'ctx'), None, 'head'), parts along dimension 0, may hold values from -360 to 360
- latent_pages: bfloat16 [16, 8, 64, 576], P(('groups', 'ctx'), 'head'), parts along dimension 0, may hold values from -6 to 6
- page_scales: bfloat16 [16, 8, 4, 64], P(('groups', 'ctx'), 'head'), parts along dimension 0, may hold values from 0.5 to 2
- page_table: int32 [16, 8], P(('groups', 'ctx')), parts along dimension 0, may hold values from 0 to 7, each once within a row
- lengths: int32 [16], P(('groups', 'ctx')), parts along dimension 0, may hold values from 128 to 512, as said below
- w_keys: bfloat16 [512, 64, 128], P('ctx', 'head'), may hold values from -0.5 to 0.5
- w_values: bfloat16 [512, 64, 128], P('ctx', 'head'), may hold values from -1 to 1
Outputs:
- attended: bfloat16 [16, 128, 64, 128], P(('groups', 'ctx'), None, 'head'), parts along dimension 0
There are 2 independent parts, one for each index of `groups`. A program takes and returns all parts, laid end to end along the dimension named above; an argument that names none is the same for every part. Nothing has to cross between parts.
Inputs may be any that keep to these rules, and one draw needn't show every extreme that they name: `page_table`: each row is a permutation of 0 to 7. `lengths`: a length counts the cached tokens and the 128 rows of the span, which take the last positions; the longest request of a part has exactly 512 tokens.
All inputs are finite; a program needn't handle non-finite values.
Results may differ from a plain program's by a relative error of at most 0.0084.
Values may be sent and summed in bfloat16 or wider, within the bound.
A program may use at most 64 MiB of HBM per device.

v0:
```python
import functools
import math

import jax
import jax.numpy as jnp
from jax import lax
from jax.experimental import pallas as pl
from jax.experimental.pallas import tpu as pltpu
from jax.sharding import PartitionSpec as P

NEGATIVE = -1e30
MESH = pl.DeviceIdType.MESH
PAIR = 4
LAG = 1


def attend_block(
    running, span_query, page_data, page_factor, first_key, row_offset, up_keys, up_values
):
    row_top, row_total, summed = running
    latent_width = up_keys.shape[0]
    group_count = page_factor.shape[1]
    page_rows = page_data.shape[1]
    key_count = page_data.shape[0] * page_rows
    head_count = span_query.shape[1]
    code_values = page_data[:, :, :latent_width].astype(jnp.float32)
    code_values = code_values.reshape(
        page_data.shape[0], page_rows, group_count, latent_width // group_count
    )
    factor = jnp.swapaxes(page_factor, 1, 2).astype(jnp.float32)[..., None]
    latent = (code_values * factor).reshape(key_count, latent_width).astype(jnp.bfloat16)
    rotary = page_data[:, :, latent_width:].reshape(key_count, -1)
    key_nope = jnp.dot(latent, up_keys, preferred_element_type=jnp.float32).astype(jnp.bfloat16)
    key_nope = key_nope.reshape(key_count, head_count, -1)
    value_rows = jnp.dot(latent, up_values, preferred_element_type=jnp.float32).astype(jnp.bfloat16)
    value_rows = value_rows.reshape(key_count, head_count, -1)
    nope_width = key_nope.shape[2]
    scores = jnp.einsum(
        "chn,khn->hck", span_query[:, :, :nope_width], key_nope, preferred_element_type=jnp.float32
    )
    scores = scores + jnp.einsum(
        "chr,kr->hck", span_query[:, :, nope_width:], rotary, preferred_element_type=jnp.float32
    )
    scores = scores * (1.0 / math.sqrt(span_query.shape[2]))
    row_position = lax.broadcasted_iota(jnp.int32, (span_query.shape[0], key_count), 0)
    key_position = first_key + lax.broadcasted_iota(jnp.int32, (span_query.shape[0], key_count), 1)
    visible = (key_position <= row_offset + row_position)[None]
    new_top = jnp.maximum(row_top, jnp.max(jnp.where(visible, scores, NEGATIVE), axis=2))
    raw_weight = jnp.where(visible, jnp.exp(scores - new_top[..., None]), 0.0)
    rescale = jnp.exp(row_top - new_top)
    row_total = row_total * rescale + jnp.sum(raw_weight, axis=2)
    weights = raw_weight.astype(jnp.bfloat16)
    summed = summed * jnp.swapaxes(rescale, 0, 1)[..., None] + jnp.einsum(
        "hck,khv->chv", weights, value_rows, preferred_element_type=jnp.float32
    )
    return (new_top, row_total, summed)


def sweep(span_query, row_offset, first_block, stop_block, fetch, up_keys, up_values):
    row_count = span_query.shape[0]
    head_count = span_query.shape[1]
    value_width = up_values.shape[1] // head_count
    initial = (
        jnp.full((head_count, row_count), NEGATIVE, jnp.float32),
        jnp.zeros((head_count, row_count), jnp.float32),
        jnp.zeros((row_count, head_count, value_width), jnp.float32),
    )

    def advance(block_index, running):
        page_data, page_factor, first_key = fetch(block_index)
        return attend_block(
            running, span_query, page_data, page_factor, first_key, row_offset, up_keys, up_values
        )

    return lax.fori_loop(first_block, stop_block, advance, initial)


def finish(row_total, summed):
    return (summed / jnp.swapaxes(row_total, 0, 1)[..., None]).astype(jnp.bfloat16)[None]


def on_device(queries, latent_pages, page_scales, page_table, lengths, w_keys, w_values):
    pool_pages, pool_scales = (
        lax.all_gather(latent_pages, "head", axis=1, tiled=True),
        lax.all_gather(page_scales, "head", axis=1, tiled=True),
    )
    full_keys, full_values = (
        lax.all_gather(w_keys, "ctx", axis=0, tiled=True),
        lax.all_gather(w_values, "ctx", axis=0, tiled=True),
    )
    latent_width = full_keys.shape[0]
    up_keys = full_keys.reshape(latent_width, -1)
    up_values = full_values.reshape(latent_width, -1)
    span_query = queries[0]
    own_pages = pool_pages[0]
    own_scales = pool_scales[0]
    own_table = page_table[0]
    row_count = span_query.shape[0]
    block_keys = 2 * own_pages.shape[1]
    own_length = lengths[0]
    block_count = (own_length + block_keys - 1) // block_keys

    def own_fetch(block_index):
        pool_slots = lax.dynamic_slice_in_dim(own_table, 2 * block_index, 2)
        return (
            jnp.take(own_pages, pool_slots, axis=0),
            jnp.take(own_scales, pool_slots, axis=0),
            block_index * block_keys,
        )

    row_top, row_total, summed = sweep(
        span_query, own_length - row_count, 0, block_count, own_fetch, up_keys, up_values
    )
    return finish(row_total, summed)


def gather_attend(
    shard_columns, q_in, k_in, t_in, w_in, out, q_rx, q_own, k_all, t_rx, w_all, rot, late, stage,
    own_sem, core_send, core_recv, relay_send, relay_recv, k_send, k_recv, t_send, t_recv,
    q_send, q_recv, z_send, z_recv, x_send, x_recv, f_send, f_recv,
    r_send, g_send, o_send, o_recv
):
    chunk_count = w_in.shape[1]
    latent_width = w_all.shape[2] * w_all.shape[3]
    span = q_in.shape[-1]
    nope = w_all.shape[-1] // 2
    rope = q_in.shape[-2] - nope
    key_count = k_all.shape[1] * k_all.shape[2]
    scale = 1.0 / math.sqrt(nope + rope)
    y, ctx, core = lax.axis_index("groups"), lax.axis_index("ctx"), lax.axis_index("head")
    row, side = ctx // 2, lax.rem(ctx, 2)
    y_peer = {"groups": 1 - y}
    core_peer = {"head": 1 - core}
    x_peer = {"ctx": 2 * row + 1 - side}

    def z_index(offset):
        return 2 * lax.rem(row + offset, shard_columns) + side

    barrier = pltpu.get_barrier_semaphore()
    peers = [y_peer, core_peer, x_peer] + [{"ctx": z_index(d)} for d in range(1, shard_columns)]
    for peer in peers:
        pl.semaphore_signal(barrier, inc=1, device_id=peer, device_id_type=MESH)
    pl.semaphore_wait(barrier, len(peers))

    def remote(source, target, send, recv, peer):
        return pltpu.make_async_remote_copy(
            src_ref=source, dst_ref=target, send_sem=send, recv_sem=recv,
            device_id=peer, device_id_type=MESH,
        )

    k_copy = remote(k_in, k_all.at[y, core], k_send, k_recv, y_peer)
    t_copy = remote(t_in, t_rx, t_send, t_recv, y_peer)
    core_copy = remote(k_in, k_all.at[y, core], core_send, core_recv, core_peer)
    relay_copy = remote(
        k_all.at[1 - y, core], k_all.at[1 - y, core], relay_send, relay_recv, core_peer
    )
    k_own = pltpu.make_async_copy(k_in, k_all.at[y, core], own_sem.at[0])
    w_own = pltpu.make_async_copy(w_in.at[y], w_all.at[:, :, ctx], own_sem.at[1])

    q_mine = pltpu.make_async_copy(q_in.at[y], q_own, own_sem.at[2])
    last = shard_columns - 1
    partner = row + 1 - 2 * lax.rem(row, 2)

    others = [row + step * d for d in range(1, shard_columns) for step in (1, -1)]

    def exists(other):
        return jnp.logical_and(other >= 0, other <= last)

    def onward(source):
        return jnp.where(source < row, row + 1, row - 1)

    def block(c, source_row, source_side):
        return w_all.at[c, :, 2 * source_row + source_side]

    def q_copy(c):
        return remote(q_in.at[1 - y, c], q_rx.at[c], q_send.at[c], q_recv.at[c], y_peer)

    def z_copy(c, step):
        return remote(
            w_in.at[y, c], block(c, row, side), z_send.at[c, (step + 1) // 2], z_recv.at[c, row],
            {"ctx": 2 * (row + step) + side},
        )

    def z_arrival(c, source):
        return remote(
            w_in.at[y, c], block(c, source, side), z_send.at[c, 0], z_recv.at[c, source], x_peer
        )

    def r_copy(c, source):
        moved = block(c, source, side)
        return remote(
            moved, moved, r_send.at[c, source], z_recv.at[c, source],
            {"ctx": 2 * onward(source) + side},
        )

    def x_copy(c):
        return remote(w_in.at[y, c], block(c, row, side), x_send.at[c], x_recv.at[c], x_peer)

    def x_arrival(c):
        return remote(w_in.at[y, c], block(c, row, 1 - side), x_send.at[c], x_recv.at[c], x_peer)

    def f_copy(c, source):
        moved = block(c, source, side)
        return remote(moved, moved, f_send.at[c, source], f_recv.at[c, source], x_peer)

    def f_arrival(c, source):
        moved = block(c, source, 1 - side)
        return remote(moved, moved, f_send.at[c, source], f_recv.at[c, source], x_peer)

    def g_copy(c):
        moved = block(c, row, 1 - side)
        return remote(
            moved, moved, g_send.at[c], f_recv.at[c, row], {"ctx": 2 * partner + side}
        )

    def over_x(c, source):
        return jnp.logical_or(lax.rem(c, 2) == 0, source != partner)

    def o_copy(c):
        return remote(stage.at[c], out.at[y, c], o_send.at[c], o_recv.at[c], y_peer)

    k_copy.start()
    t_copy.start()
    core_copy.start()
    k_own.start()
    q_mine.start()
    w_own.start()

    def begin(c, carry):
        for step in (1, -1):
            @pl.when(exists(row + step))
            def _():
                z_copy(c, step).start()

        x_copy(c).start()
        q_copy(c).start()
        return carry

    lax.fori_loop(0, chunk_count, begin, 0)
    k_own.wait()
    w_own.wait()
    q_mine.wait()
    def settle():
        t_copy.wait_recv()
        core_copy.wait_recv()
        relay_copy.wait_recv()
        page = key_count // t_in.shape[1]
        offset = lax.broadcasted_iota(jnp.int32, (page, span), 0)
        offset = offset - lax.broadcasted_iota(jnp.int32, (page, span), 1)
        for request, t_ref in ((y, t_in), (1 - y, t_rx)):
            rot[request] = k_all[request, :, :, latent_width:].reshape(key_count, rope)
            late[request] = jnp.concatenate(
                [t_ref[0:1, p : p + 1] + offset for p in range(t_in.shape[1])], axis=0
            )

    def attend(c, request, q_ref, put):
        latent = k_all[request, :, :, :latent_width].reshape(key_count, latent_width)
        visible = late[request] <= 0
        for h in range(PAIR):
            weight = w_all[c, h].reshape(latent_width, -1)
            up = jnp.dot(latent, weight, preferred_element_type=jnp.float32).astype(jnp.bfloat16)
            keys = jnp.concatenate([up[:, :nope], rot[request]], axis=1)
            scores = jnp.dot(keys, q_ref[h], preferred_element_type=jnp.float32)
            scores = jnp.where(visible, scores * scale, NEGATIVE)
            top = jnp.max(scores, axis=0, keepdims=True)
            raw = jnp.where(visible, jnp.exp(scores - top), 0.0)
            total = jnp.sum(raw, axis=0, keepdims=True)
            summed = lax.dot_general(
                up[:, nope:], raw.astype(jnp.bfloat16), (((0,), (0,)), ((), ())),
                preferred_element_type=jnp.float32,
            )
            put(h, jnp.transpose(summed / total).astype(jnp.bfloat16))

    def advance(c, carry):
        @pl.when(c < chunk_count)
        def _():
            x_arrival(c).wait_recv()

            @pl.when(lax.rem(c, 2) == 1)
            def _():
                g_copy(c).start()

            for source in others:
                @pl.when(exists(source))
                def _():
                    z_arrival(c, source).wait_recv()

                    @pl.when(exists(onward(source)))
                    def _():
                        r_copy(c, source).start()

                    @pl.when(over_x(c, source))
                    def _():
                        f_copy(c, source).start()

        @pl.when(c == 0)
        def _():
            k_copy.wait_recv()
            relay_copy.start()

        @pl.when(c == LAG)
        def _():
            settle()

        @pl.when(c >= LAG)
        def _():
            b = c - LAG
            for d in range(1, shard_columns):
                f_arrival(b, lax.rem(row + d, shard_columns)).wait_recv()
            q_copy(b).wait_recv()

            def put_stage(h, value):
                stage[b, h] = value

            def put_out(h, value):
                out[y, b, h] = value

            attend(b, 1 - y, q_rx.at[b], put_stage)
            attend(b, y, q_own.at[b], put_out)
            o_copy(b).start()

        return carry

    lax.fori_loop(0, chunk_count + LAG, advance, 0)
    k_copy.wait_send()
    t_copy.wait_send()
    core_copy.wait_send()
    relay_copy.wait_send()

    def end(c, carry):
        q_copy(c).wait_send()
        x_copy(c).wait_send()
        for d in range(1, shard_columns):
            other = lax.rem(row + d, shard_columns)

            @pl.when(over_x(c, other))
            def _():
                f_copy(c, other).wait_send()

            @pl.when(exists(onward(other)))
            def _():
                r_copy(c, other).wait_send()

        for step in (1, -1):
            @pl.when(exists(row + step))
            def _():
                z_copy(c, step).wait_send()

        @pl.when(lax.rem(c, 2) == 1)
        def _():
            g_copy(c).wait_send()

        o_copy(c).wait()
        return carry

    lax.fori_loop(0, chunk_count, end, 0)


def shared_on_device(
    shards, queries, latent_pages, page_scales, page_table, lengths, w_keys, w_values
):
    _, span, heads, _ = queries.shape
    latent_rows, _, nope = w_keys.shape
    _, slots, page, width = latent_pages.shape
    latent_width = latent_rows * shards
    rope = width - latent_width
    groups = page_scales.shape[2]
    chunks = heads // (2 * PAIR)
    keys = slots * page
    columns = shards // 2
    w_in = jnp.concatenate([jnp.swapaxes(w_keys, 0, 1), jnp.swapaxes(w_values, 0, 1)], axis=-1)
    w_in = w_in.reshape(2, chunks, PAIR, latent_rows, 2 * nope)
    q_in = jnp.transpose(queries[0], (1, 2, 0)).reshape(2, chunks, PAIR, -1, span)
    codes = latent_pages[0, :, :, :latent_width].astype(jnp.float32)
    codes = codes.reshape(slots, page, groups, latent_width // groups)
    factor = jnp.swapaxes(page_scales[0], 1, 2).astype(jnp.float32)[..., None]
    latent = (codes * factor).reshape(keys, latent_width).astype(jnp.bfloat16)
    rotary = latent_pages[0, :, :, latent_width:].reshape(keys, rope)
    k_in = jnp.concatenate([latent, rotary], axis=1)
    pool = page_table.shape[1]
    places = jnp.arange(pool, dtype=jnp.int32)
    order = jnp.sum(jnp.where(page_table[0][:, None] == places[None], places[:, None], 0), axis=0)
    t_in = jnp.broadcast_to((order * page - (lengths[0] - span))[None], (8, pool))
    dma, vmem = pltpu.SemaphoreType.DMA, pltpu.VMEM
    bf16 = jnp.bfloat16
    out = pl.pallas_call(
        functools.partial(gather_attend, columns),
        out_shape=jax.ShapeDtypeStruct((2, chunks, PAIR, span, nope), bf16),
        in_specs=[pl.BlockSpec(memory_space=pl.ANY)] + [pl.BlockSpec(memory_space=vmem)] * 3,
        out_specs=pl.BlockSpec(memory_space=vmem),
        scratch_shapes=[
            vmem(q_in.shape[1:], bf16),
            vmem(q_in.shape[1:], bf16),
            vmem((2, 2, keys, k_in.shape[1]), bf16),
            vmem(t_in.shape, jnp.int32),
            vmem((chunks, PAIR, shards, latent_rows, 2 * nope), bf16),
            vmem((2, 2 * keys, rope), bf16),
            vmem((2, 2 * keys, span), jnp.int32),
            vmem((chunks, PAIR, span, nope), bf16),
            dma((3,)), dma, dma, dma, dma, dma, dma, dma, dma,
            dma((chunks,)), dma((chunks,)),
            dma((chunks, 2)), dma((chunks, columns)),
            dma((chunks,)), dma((chunks,)),
            dma((chunks, columns)), dma((chunks, columns)),
            dma((chunks, columns)), dma((chunks,)), dma((chunks,)), dma((chunks,)),
        ],
        compiler_params=pltpu.CompilerParams(
            collective_id=0, has_side_effects=True, vmem_limit_bytes=48 * 1024 * 1024
        ),
    )(q_in, k_in, t_in, w_in)
    return jnp.swapaxes(out.reshape(heads, span, nope), 0, 1)[None]


def body_for(mesh, queries, latent_pages, page_scales, page_table, lengths, w_keys, w_values):
    args = (queries, latent_pages, page_scales, page_table, lengths, w_keys, w_values)
    shards = mesh.shape["ctx"]
    rope = latent_pages.shape[3] - w_keys.shape[0] * shards
    fits = (
        mesh.shape["groups"] == 2 and mesh.shape["head"] == 2 and shards % 4 == 0
        and shards >= 8 and w_keys.shape[0] % 16 == 0 and queries.shape[2] % (2 * PAIR) == 0
        and w_keys.shape == w_values.shape and 2 * rope == w_keys.shape[2]
    )
    if fits:
        return shared_on_device(shards, *args)
    return on_device(*args)


def solution(mesh):
    return jax.shard_map(
        functools.partial(body_for, mesh),
        mesh=mesh,
        in_specs=(
            P(("groups", "ctx"), None, "head", None),
            P(("groups", "ctx"), "head", None, None),
            P(("groups", "ctx"), "head", None, None),
            P(("groups", "ctx"), None),
            P(("groups", "ctx")),
            P("ctx", "head", None),
            P("ctx", "head", None),
        ),
        out_specs=P(("groups", "ctx"), None, "head", None),
        check_vma=False,
    )
```

profile of v0, /device:TPU:0, one launch (start us, length us, event | category | flops | bytes accessed | tf_op | source)
XLA Modules:
  0.0 71.4 jit_solution(5595060348822097087)
XLA Ops:
  0.0 0.0 slice-start.1
  0.0 0.0 slice-start
  0.7 0.7 %select_reduce_fusion = s32[8]{0:T(128)S(1)} fusion(s32[8]{0:T(128)} %bitcast.38), kind=kLoop, calls=%fused_computation.6 | loop fusion | flops 184 | bytes 64 | tf_op jit(solution)/shard_map/reduce_sum | solution.py:382
  1.5 0.7 convert_bitcast_fusion
  2.1 0.0 copy-start.1
  2.1 0.0 copy-start.2
  2.2 0.1 copy.11
  2.3 0.3 mul.18
  2.6 0.0 slice-done.1
  2.6 0.1 fusion
  2.7 0.0 slice-done
  2.8 0.4 copy-done.1
  3.2 0.2 copy-done.2
  3.3 0.1 pad_maximum_fusion
  3.5 0.0 copy-start
  3.5 0.6 copy.12
  4.1 0.8 %copy-done = bf16[1,128,32,192]{1,3,2,0:T(8,128)(2,1)S(1)} copy-done((bf16[1,128,32,192]{1,3,2,0:T(8,128)(2,1)S(1)}, bf16[1,128,32,192]{1,3,2,0:T(8,128)(2,1)}, u32[]{:S(2)}) %copy-start) | copy-done | bytes 1572888
  4.9 64.9 %shard_map.73 = bf16[2,4,4,128,128]{4,3,2,1,0:T(8,128)(2,1)S(1)} custom-call(bf16[2,4,4,192,128]{4,3,2,1,0:T(8,128)(2,1)S(1)} %bitcast.33, bf16[256,576]{1,0:T(8,128)(2,1)S(1)} %pad_maximum_fusion.1.k_in, s32[8,8]{1,0:T(8,128)S(1)} %broadcast_in_dim.26.t_in, bf16[2,4,4,64,256]{4,3,2,1,0:T(8,128)(2,1)S(1)} %bitcast.31), custom_call_target="tpu_custom_call" | custom-call | tf_op jit(solution)/shard_map/pallas_call | solution.py:386
  69.8 1.6 %copy.17 = bf16[32,128,128]{2,0,1:T(8,128)(2,1)} copy(bf16[32,128,128]{2,1,0:T(8,128)(2,1)S(1)} %bitcast.32) | data formatting | bytes 2097152 | tf_op jit(solution)/shard_map/reshape | solution.py:411
  (3 shorter events, 0.0 us)
Async XLA Ops:
  0.0 2.6 %slice-start.1 = ((bf16[1,4,64,576]{3,2,1,0:T(8,128)(2,1)}), bf16[1,4,64,512]{3,2,1,0:T(8,128)(2,1)S(1)}, s32[]{:S(2)}) async-start(bf16[1,4,64,576]{3,2,1,0:T(8,128)(2,1)} %param.8), calls=%async_computation.1 | async-start | bytes 524288 | tf_op jit(solution)/shard_map/slice | solution.py:374
  0.0 2.7 %slice-start = ((bf16[1,4,64,576]{3,2,1,0:T(8,128)(2,1)}), bf16[1,4,64,64]{3,2,1,0:T(8,128)(2,1)S(1)}, s32[]{:S(2)}) async-start(bf16[1,4,64,576]{3,2,1,0:T(8,128)(2,1)} %param.8), calls=%async_computation | async-start | bytes 131072 | tf_op jit(solution)/shard_map/slice | solution.py:378
  2.1 1.0 %copy-start.1 = (bf16[64,32,128]{2,1,0:T(8,128)(2,1)S(1)}, bf16[64,32,128]{2,1,0:T(8,128)(2,1)}, u32[]{:S(2)}) copy-start(bf16[64,32,128]{2,1,0:T(8,128)(2,1)} %param.13) | copy-start | bytes 1572868
  2.1 1.2 %copy-start.2 = (bf16[64,32,128]{2,1,0:T(8,128)(2,1)S(1)}, bf16[64,32,128]{2,1,0:T(8,128)(2,1)}, u32[]{:S(2)}) copy-start(bf16[64,32,128]{2,1,0:T(8,128)(2,1)} %param.12) | copy-start | bytes 1572868
  3.5 1.4 %copy-start = (bf16[1,128,32,192]{1,3,2,0:T(8,128)(2,1)S(1)}, bf16[1,128,32,192]{1,3,2,0:T(8,128)(2,1)}, u32[]{:S(2)}) copy-start(bf16[1,128,32,192]{1,3,2,0:T(8,128)(2,1)} %param.7) | copy-start | bytes 4718596
where the time goes:
time: 71.7 us; the launch traced here: 71.4 us
  Pallas kernels  64.9 us (91%)
  local copies, waits for them, and re-layouts  4.08 us (6%)
  other arithmetic  1.71 us (2%)
  between operations  0.78 us (1%)
    pallas_call x1, Pallas kernels, shared_on_device(): pl.pallas_call(functools.partial(gather_attend, columns), out_shape=jax.S...  64.9 us
    reshape x1, local copies, waits for them, and re-layouts, shared_on_device(): return jnp.swapaxes(out.reshape(heads, span, nope), 0, 1)[None]  1.65 us

commit v1 on v0

v1 whole, which is shorter than its diff:
```python
import functools
import math

import jax
import jax.numpy as jnp
from jax import lax
from jax.experimental import pallas as pl
from jax.experimental.pallas import tpu as pltpu
from jax.sharding import PartitionSpec as P

NEGATIVE = -1e30
MESH = pl.DeviceIdType.MESH
PAIR = 2
LAG = 2
AHEAD = 2


def attend_block(
    running, span_query, page_data, page_factor, first_key, row_offset, up_keys, up_values
):
    row_top, row_total, summed = running
    latent_width = up_keys.shape[0]
    group_count = page_factor.shape[1]
    page_rows = page_data.shape[1]
    key_count = page_data.shape[0] * page_rows
    head_count = span_query.shape[1]
    code_values = page_data[:, :, :latent_width].astype(jnp.float32)
    code_values = code_values.reshape(
        page_data.shape[0], page_rows, group_count, latent_width // group_count
    )
    factor = jnp.swapaxes(page_factor, 1, 2).astype(jnp.float32)[..., None]
    latent = (code_values * factor).reshape(key_count, latent_width).astype(jnp.bfloat16)
    rotary = page_data[:, :, latent_width:].reshape(key_count, -1)
    key_nope = jnp.dot(latent, up_keys, preferred_element_type=jnp.float32).astype(jnp.bfloat16)
    key_nope = key_nope.reshape(key_count, head_count, -1)
    value_rows = jnp.dot(latent, up_values, preferred_element_type=jnp.float32).astype(jnp.bfloat16)
    value_rows = value_rows.reshape(key_count, head_count, -1)
    nope_width = key_nope.shape[2]
    scores = jnp.einsum(
        "chn,khn->hck", span_query[:, :, :nope_width], key_nope, preferred_element_type=jnp.float32
    )
    scores = scores + jnp.einsum(
        "chr,kr->hck", span_query[:, :, nope_width:], rotary, preferred_element_type=jnp.float32
    )
    scores = scores * (1.0 / math.sqrt(span_query.shape[2]))
    row_position = lax.broadcasted_iota(jnp.int32, (span_query.shape[0], key_count), 0)
    key_position = first_key + lax.broadcasted_iota(jnp.int32, (span_query.shape[0], key_count), 1)
    visible = (key_position <= row_offset + row_position)[None]
    new_top = jnp.maximum(row_top, jnp.max(jnp.where(visible, scores, NEGATIVE), axis=2))
    raw_weight = jnp.where(visible, jnp.exp(scores - new_top[..., None]), 0.0)
    rescale = jnp.exp(row_top - new_top)
    row_total = row_total * rescale + jnp.sum(raw_weight, axis=2)
    weights = raw_weight.astype(jnp.bfloat16)
    summed = summed * jnp.swapaxes(rescale, 0, 1)[..., None] + jnp.einsum(
        "hck,khv->chv", weights, value_rows, preferred_element_type=jnp.float32
    )
    return (new_top, row_total, summed)


def sweep(span_query, row_offset, first_block, stop_block, fetch, up_keys, up_values):
    row_count = span_query.shape[0]
    head_count = span_query.shape[1]
    value_width = up_values.shape[1] // head_count
    initial = (
        jnp.full((head_count, row_count), NEGATIVE, jnp.float32),
        jnp.zeros((head_count, row_count), jnp.float32),
        jnp.zeros((row_count, head_count, value_width), jnp.float32),
    )

    def advance(block_index, running):
        page_data, page_factor, first_key = fetch(block_index)
        return attend_block(
            running, span_query, page_data, page_factor, first_key, row_offset, up_keys, up_values
        )

    return lax.fori_loop(first_block, stop_block, advance, initial)


def finish(row_total, summed):
    return (summed / jnp.swapaxes(row_total, 0, 1)[..., None]).astype(jnp.bfloat16)[None]


def on_device(queries, latent_pages, page_scales, page_table, lengths, w_keys, w_values):
    pool_pages, pool_scales = (
        lax.all_gather(latent_pages, "head", axis=1, tiled=True),
        lax.all_gather(page_scales, "head", axis=1, tiled=True),
    )
    full_keys, full_values = (
        lax.all_gather(w_keys, "ctx", axis=0, tiled=True),
        lax.all_gather(w_values, "ctx", axis=0, tiled=True),
    )
    latent_width = full_keys.shape[0]
    up_keys = full_keys.reshape(latent_width, -1)
    up_values = full_values.reshape(latent_width, -1)
    span_query = queries[0]
    own_pages = pool_pages[0]
    own_scales = pool_scales[0]
    own_table = page_table[0]
    row_count = span_query.shape[0]
    block_keys = 2 * own_pages.shape[1]
    own_length = lengths[0]
    block_count = (own_length + block_keys - 1) // block_keys

    def own_fetch(block_index):
        pool_slots = lax.dynamic_slice_in_dim(own_table, 2 * block_index, 2)
        return (
            jnp.take(own_pages, pool_slots, axis=0),
            jnp.take(own_scales, pool_slots, axis=0),
            block_index * block_keys,
        )

    row_top, row_total, summed = sweep(
        span_query, own_length - row_count, 0, block_count, own_fetch, up_keys, up_values
    )
    return finish(row_total, summed)


def gather_attend(
    shard_columns, q_in, pages_in, scales_in, table_in, wk_in, wv_in, length_in, out,
    q_rx, q_own, k_all, pages, scales, table, t_own, t_rx, wk_raw, wv_raw, w_all, rot, late,
    stage, own_sem, core_send, core_recv, relay_send, relay_recv, k_send, k_recv, t_send, t_recv,
    q_send, q_recv, z_send, z_recv, x_send, x_recv, f_send, f_recv,
    r_send, g_send, o_send, o_recv
):
    chunk_count = w_all.shape[0]
    latent_rows = w_all.shape[3]
    latent_width = w_all.shape[2] * latent_rows
    span = q_in.shape[-1]
    nope = w_all.shape[-1] // 2
    rope = q_in.shape[-2] - nope
    half_heads = chunk_count * PAIR
    page_count, page = k_all.shape[2], k_all.shape[3]
    key_count = 2 * page_count * page
    group_count = scales.shape[1]
    group_width = latent_width // group_count
    scale = 1.0 / math.sqrt(nope + rope)
    y, ctx, core = lax.axis_index("groups"), lax.axis_index("ctx"), lax.axis_index("head")
    row, side = ctx // 2, lax.rem(ctx, 2)
    last = shard_columns - 1
    y_peer = {"groups": 1 - y}
    core_peer = {"head": 1 - core}
    x_peer = {"ctx": 2 * row + 1 - side}
    partner = row + 1 - 2 * lax.rem(row, 2)

    def column(other):
        return {"ctx": 2 * other + side}

    def exists(other):
        return jnp.logical_and(other >= 0, other <= last)

    def local(source, target, index):
        return pltpu.make_async_copy(source, target, own_sem.at[index])

    heads_here = pl.ds(pl.multiple_of(y * half_heads, half_heads), half_heads)
    loads = [
        local(wk_in.at[:, heads_here], wk_raw, 0),
        local(wv_in.at[:, heads_here], wv_raw, 1),
        local(pages_in, pages, 2),
        local(scales_in, scales, 3),
        local(table_in, table, 4),
        local(q_in.at[y], q_own, 5),
    ]
    for load in loads:
        load.start()

    barrier = pltpu.get_barrier_semaphore()
    peers = [y_peer, core_peer, x_peer]
    peers += [column(lax.rem(row + d, shard_columns)) for d in range(1, shard_columns)]
    for peer in peers:
        pl.semaphore_signal(barrier, inc=1, device_id=peer, device_id_type=MESH)

    def remote(source, target, send, recv, peer):
        return pltpu.make_async_remote_copy(
            src_ref=source, dst_ref=target, send_sem=send, recv_sem=recv,
            device_id=peer, device_id_type=MESH,
        )

    def moved(c, source_row, source_side, send, recv, peer):
        block = w_all.at[c, :, 2 * source_row + source_side]
        return remote(block, block, send, recv, peer)

    k_mine = k_all.at[y, core]
    k_copy = remote(k_mine, k_mine, k_send, k_recv, y_peer)
    t_copy = remote(t_own, t_rx, t_send, t_recv, y_peer)
    core_copy = remote(k_mine, k_mine, core_send, core_recv, core_peer)
    k_other = k_all.at[1 - y, core]
    relay_copy = remote(k_other, k_other, relay_send, relay_recv, core_peer)

    def q_copy(c):
        return remote(q_in.at[1 - y, c], q_rx.at[c], q_send.at[c], q_recv.at[c], y_peer)

    hops = [(distance, step) for distance in (1, 2) for step in (1, -1)]

    def z_copy(c, index):
        distance, step = hops[index]
        return moved(
            c, row, side, z_send.at[c, index], z_recv.at[c, row], column(row + step * distance)
        )

    def z_arrival(c, source):
        return moved(c, source, side, z_send.at[c, 0], z_recv.at[c, source], x_peer)

    def r_copy(c, step):
        source = row + 2 * step
        return moved(c, source, side, r_send.at[c], z_recv.at[c, source], column(row - step))

    def x_copy(c):
        return moved(c, row, side, x_send.at[c], x_recv.at[c], x_peer)

    def x_arrival(c):
        return moved(c, row, 1 - side, x_send.at[c], x_recv.at[c], x_peer)

    def f_copy(c, source):
        return moved(c, source, side, f_send.at[c, source], f_recv.at[c, source], x_peer)

    def f_arrival(c, source):
        return moved(c, source, 1 - side, f_send.at[c, source], f_recv.at[c, source], x_peer)

    def g_copy(c):
        return moved(c, row, 1 - side, g_send.at[c], f_recv.at[c, row], column(partner))

    def by_z(c):
        return lax.rem(c, 2) == 1

    def over_x(c, source):
        return jnp.logical_or(jnp.logical_not(by_z(c)), source != partner)

    def o_copy(c):
        return remote(stage.at[c], out.at[y, c], o_send.at[c], o_recv.at[c], y_peer)

    def send_own(c):
        for index, (distance, step) in enumerate(hops):
            @pl.when(exists(row + step * distance))
            def _():
                z_copy(c, index).start()

        x_copy(c).start()

    loads[0].wait()
    loads[1].wait()
    keys_by_head = jnp.swapaxes(wk_raw[...], 0, 1)
    values_by_head = jnp.swapaxes(wv_raw[...], 0, 1)
    for c in range(chunk_count):
        for h in range(PAIR):
            w_all[c, h, ctx, :, :nope] = keys_by_head[c * PAIR + h]
            w_all[c, h, ctx, :, nope:] = values_by_head[c * PAIR + h]

    pl.semaphore_wait(barrier, len(peers))
    for c in range(AHEAD):
        send_own(c)

    loads[2].wait()
    loads[3].wait()
    columns = jnp.transpose(
        scales[...].astype(jnp.float32).reshape(page_count * group_count, page)
    )
    for p in range(page_count):
        for g in range(group_count):
            part = pl.ds(g * group_width, group_width)
            at = p * group_count + g
            codes = pages[p, :, part].astype(jnp.float32)
            k_all[y, core, p, :, part] = (codes * columns[:, at : at + 1]).astype(jnp.bfloat16)
        k_all[y, core, p, :, latent_width:] = pages[p, :, latent_width:]
    k_copy.start()
    core_copy.start()
    loads[4].wait()
    slots = 2 * page_count
    slot = lax.broadcasted_iota(jnp.int32, (slots, slots), 0)
    place = lax.broadcasted_iota(jnp.int32, (slots, slots), 1)
    order = jnp.sum(jnp.where(table[...] == slot, place, 0), axis=1, keepdims=True)
    t_own[...] = jnp.broadcast_to(order * page - (length_in[0] - span), t_own.shape)
    t_copy.start()

    def send_queries(c, carry):
        q_copy(c).start()
        return carry

    lax.fori_loop(0, chunk_count, send_queries, 0)
    loads[5].wait()

    def settle():
        t_copy.wait_recv()
        core_copy.wait_recv()
        relay_copy.wait_recv()
        offset = lax.broadcasted_iota(jnp.int32, (page, span), 0)
        offset = offset - lax.broadcasted_iota(jnp.int32, (page, span), 1)
        for request, t_ref in ((y, t_own), (1 - y, t_rx)):
            rot[request] = k_all[request, :, :, :, latent_width:].reshape(key_count, rope)
            late[request] = jnp.concatenate(
                [t_ref[p : p + 1] + offset for p in range(slots)], axis=0
            )

    def attend(c, h, request, q_ref):
        latent = k_all[request, :, :, :, :latent_width].reshape(key_count, latent_width)
        visible = late[request] <= 0
        weight = w_all[c, h].reshape(latent_width, -1)
        up = jnp.dot(latent, weight, preferred_element_type=jnp.float32).astype(jnp.bfloat16)
        keys = jnp.concatenate([up[:, :nope], rot[request]], axis=1)
        scores = jnp.dot(keys, q_ref[c, h], preferred_element_type=jnp.float32)
        scores = jnp.where(visible, scores * scale, NEGATIVE)
        top = jnp.max(scores, axis=0, keepdims=True)
        raw = jnp.where(visible, jnp.exp(scores - top), 0.0)
        total = jnp.sum(raw, axis=0, keepdims=True)
        summed = lax.dot_general(
            up[:, nope:], raw.astype(jnp.bfloat16), (((0,), (0,)), ((), ())),
            preferred_element_type=jnp.float32,
        )
        return jnp.transpose(summed / total).astype(jnp.bfloat16)

    def pass_on(c, distance):
        for step in (1, -1):
            source = row + step * distance

            @pl.when(exists(source))
            def _():
                z_arrival(c, source).wait_recv()
                if distance == 2:
                    @pl.when(exists(row - step))
                    def _():
                        r_copy(c, step).start()

                @pl.when(over_x(c, source))
                def _():
                    f_copy(c, source).start()

    def advance(c, carry):
        @pl.when(c + AHEAD < chunk_count)
        def _():
            send_own(c + AHEAD)

        sending = c < chunk_count
        ready = c >= LAG
        b = jnp.maximum(c - LAG, 0)
        for unit in range(2 * PAIR):
            if unit == 0:
                @pl.when(sending)
                def _():
                    pass_on(c, 1)
                    x_arrival(c).wait_recv()

                    @pl.when(by_z(c))
                    def _():
                        g_copy(c).start()
            elif unit < shard_columns - 1:
                @pl.when(sending)
                def _():
                    pass_on(c, unit + 1)

            if unit == shard_columns - 2:
                @pl.when(c == 1)
                def _():
                    k_copy.wait_recv()
                    relay_copy.start()

            if unit == 0:
                @pl.when(c == LAG)
                def _():
                    settle()

            @pl.when(ready)
            def _():
                if unit == 0:
                    for d in range(1, shard_columns):
                        f_arrival(b, lax.rem(row + d, shard_columns)).wait_recv()
                    q_copy(b).wait_recv()
                h = unit % PAIR
                if unit < PAIR:
                    stage[b, h] = attend(b, h, 1 - y, q_rx)
                    if unit == PAIR - 1:
                        o_copy(b).start()
                else:
                    out[y, b, h] = attend(b, h, y, q_own)

        return carry

    lax.fori_loop(0, chunk_count + LAG, advance, 0)
    k_copy.wait_send()
    t_copy.wait_send()
    core_copy.wait_send()
    relay_copy.wait_send()

    def end(c, carry):
        q_copy(c).wait_send()
        x_copy(c).wait_send()
        for index, (distance, step) in enumerate(hops):
            @pl.when(exists(row + step * distance))
            def _():
                z_copy(c, index).wait_send()

            if distance == 2:
                @pl.when(jnp.logical_and(exists(row + 2 * step), exists(row - step)))
                def _():
                    r_copy(c, step).wait_send()

        for d in range(1, shard_columns):
            other = lax.rem(row + d, shard_columns)

            @pl.when(over_x(c, other))
            def _():
                f_copy(c, other).wait_send()

        @pl.when(by_z(c))
        def _():
            g_copy(c).wait_send()

        return carry

    lax.fori_loop(0, chunk_count, end, 0)

    def end_out(c, carry):
        o_copy(c).wait()
        return carry

    lax.fori_loop(0, chunk_count, end_out, 0)


def shared_on_device(
    shards, queries, latent_pages, page_scales, page_table, lengths, w_keys, w_values
):
    _, span, heads, _ = queries.shape
    latent_rows, _, nope = w_keys.shape
    _, slots, page, width = latent_pages.shape
    latent_width = latent_rows * shards
    rope = width - latent_width
    groups = page_scales.shape[2]
    chunks = heads // (2 * PAIR)
    pool = page_table.shape[1]
    columns = shards // 2
    half = heads // 2
    q_in = jnp.transpose(queries[0], (1, 2, 0)).reshape(2, chunks, PAIR, -1, span)
    operands = (
        q_in, latent_pages[0], page_scales[0], page_table, w_keys, w_values
    )
    dma, vmem = pltpu.SemaphoreType.DMA, pltpu.VMEM
    bf16, int32 = jnp.bfloat16, jnp.int32
    out = pl.pallas_call(
        functools.partial(gather_attend, columns),
        out_shape=vmem((2, chunks, PAIR, span, nope), bf16),
        in_specs=[pl.BlockSpec(memory_space=pltpu.HBM)] * 6
        + [pl.BlockSpec(memory_space=pltpu.SMEM)],
        out_specs=pl.BlockSpec(memory_space=vmem),
        scratch_shapes=[
            vmem(q_in.shape[1:], bf16),
            vmem(q_in.shape[1:], bf16),
            vmem((2, 2, slots, page, width), bf16),
            vmem((slots, page, width), bf16),
            vmem((slots, groups, page), bf16),
            vmem((1, pool), int32),
            vmem((pool, span), int32),
            vmem((pool, span), int32),
            vmem((latent_rows, half, nope), bf16),
            vmem((latent_rows, half, nope), bf16),
            vmem((chunks, PAIR, shards, latent_rows, 2 * nope), bf16),
            vmem((2, pool * page, rope), bf16),
            vmem((2, pool * page, span), int32),
            vmem((chunks, PAIR, span, nope), bf16),
            dma((6,)), dma, dma, dma, dma, dma, dma, dma, dma,
            dma((chunks,)), dma((chunks,)),
            dma((chunks, 4)), dma((chunks, columns)),
            dma((chunks,)), dma((chunks,)),
            dma((chunks, columns)), dma((chunks, columns)),
            dma((chunks,)), dma((chunks,)), dma((chunks,)), dma((chunks,)),
        ],
        compiler_params=pltpu.CompilerParams(
            collective_id=0, has_side_effects=True, vmem_limit_bytes=48 * 1024 * 1024
        ),
    )(*(pltpu.with_memory_space_constraint(x, pltpu.HBM) for x in operands), lengths)
    return jnp.swapaxes(out.reshape(heads, span, nope), 0, 1)[None]


def body_for(mesh, queries, latent_pages, page_scales, page_table, lengths, w_keys, w_values):
    args = (queries, latent_pages, page_scales, page_table, lengths, w_keys, w_values)
    shards = mesh.shape["ctx"]
    rope = latent_pages.shape[3] - w_keys.shape[0] * shards
    fits = (
        mesh.shape["groups"] == 2 and mesh.shape["head"] == 2 and shards == 8
        and w_keys.shape[0] % 16 == 0 and queries.shape[2] % 16 == 0
        and w_keys.shape == w_values.shape and 2 * rope == w_keys.shape[2]
    )
    if fits:
        return shared_on_device(shards, *args)
    return on_device(*args)


def solution(mesh):
    return jax.shard_map(
        functools.partial(body_for, mesh),
        mesh=mesh,
        in_specs=(
            P(("groups", "ctx"), None, "head", None),
            P(("groups", "ctx"), "head", None, None),
            P(("groups", "ctx"), "head", None, None),
            P(("groups", "ctx"), None),
            P(("groups", "ctx")),
            P("ctx", "head", None),
            P("ctx", "head", None),
        ),
        out_specs=P(("groups", "ctx"), None, "head", None),
        check_vma=False,
    )
```

time: 71.7 us -> 63.7 us (0.89)
  Pallas kernels: 64.9 us -> 61.2 us
  local copies, waits for them, and re-layouts: 4.08 us -> 1.65 us
  other arithmetic: 1.71 us -> 0 us
    pallas_call x1, Pallas kernels: 64.9 us -> 61.2 us  [shared_on_device(): pl.pallas_call(functools.partial(gather_attend, columns), out_shape=vmem(...]
    unnamed x6 -> x0, local copies, waits for them, and re-layouts: 1.38 us -> none
    convert_element_type x2 -> x0, other arithmetic: 0.79 us -> none  [the longest x1 0.69 us: shared_on_device(): factor = jnp.swapaxes(page_scales[0], 1, 2).astype(jnp.float32)[..., None]]
    reduce_sum x1 -> x0, other arithmetic: 0.74 us -> none  [shared_on_device(): jnp.sum(jnp.where(page_table[0][:, None] == places[None], places[:, None]...]
where the time goes in v1:
time: 63.7 us; the launch traced here: 63.5 us
  Pallas kernels  61.2 us (96%)
  local copies, waits for them, and re-layouts  1.65 us (3%)
  between operations  0.66 us (1%)
    pallas_call x1, Pallas kernels, shared_on_device(): pl.pallas_call(functools.partial(gather_attend, columns), out_shape=vmem(...  61.2 us
    reshape x1, local copies, waits for them, and re-layouts, shared_on_device(): return jnp.swapaxes(out.reshape(heads, span, nope), 0, 1)[None]  1.65 us

profile of v1, /device:TPU:0, one launch (start us, length us, event | category | flops | bytes accessed | tf_op | source)
XLA Modules:
  0.0 63.5 jit_solution(296975917222994654)
XLA Ops:
  0.7 61.2 %shard_map.73 = bf16[2,8,2,128,128]{4,3,2,1,0:T(8,128)(2,1)S(1)} custom-call(bf16[2,8,2,192,128]{4,3,2,1,0:T(8,128)(2,1)} %bitcast.14, bf16[4,64,576]{2,1,0:T(8,128)(2,1)} %bitcast.15, bf16[4,4,64]{2,1,0:T(4,128)(2,1)} %bitcast.16, s32[1,8]{1,0:T(1,128)} %table_in.1, bf16[64,32,128]{2,1,0:T(8,128)(2,1)} %wk_in.1, bf16[64,32,128]{2,1,0:T(8,128)(2,1)} %wv_in.1, ...), custom_call_target="tpu_custom_call" | custom-call | tf_op jit(solution)/shard_map/pallas_call | solution.py:436
  61.9 1.6 %copy.10 = bf16[32,128,128]{2,0,1:T(8,128)(2,1)} copy(bf16[32,128,128]{2,1,0:T(8,128)(2,1)S(1)} %bitcast.13) | data formatting | bytes 2097152 | tf_op jit(solution)/shard_map/reshape | solution.py:468

commit v2 on v1

--- a/solution.py
+++ b/solution.py
@@ -12,7 +12,7 @@
 MESH = pl.DeviceIdType.MESH
 PAIR = 2
 LAG = 2
-AHEAD = 2
+AHEAD = 3
 
 
 def attend_block(
@@ -187,46 +187,51 @@
     relay_copy = remote(k_other, k_other, relay_send, relay_recv, core_peer)
 
     def q_copy(c):
-        return remote(q_in.at[1 - y, c], q_rx.at[c], q_send.at[c], q_recv.at[c], y_peer)
+        return remote(q_in.at[1 - y, c], q_rx.at[c], q_send, q_recv.at[c], y_peer)
 
     hops = [(distance, step) for distance in (1, 2) for step in (1, -1)]
 
     def z_copy(c, index):
         distance, step = hops[index]
         return moved(
-            c, row, side, z_send.at[c, index], z_recv.at[c, row], column(row + step * distance)
+            c, row, side, z_send.at[index], z_recv.at[c, row], column(row + step * distance)
         )
 
     def z_arrival(c, source):
-        return moved(c, source, side, z_send.at[c, 0], z_recv.at[c, source], x_peer)
+        return moved(c, source, side, z_send.at[0], z_recv.at[c, source], x_peer)
 
     def r_copy(c, step):
         source = row + 2 * step
-        return moved(c, source, side, r_send.at[c], z_recv.at[c, source], column(row - step))
+        return moved(c, source, side, r_send, z_recv.at[c, source], column(row - step))
 
     def x_copy(c):
-        return moved(c, row, side, x_send.at[c], x_recv.at[c], x_peer)
+        return moved(c, row, side, x_send, x_recv.at[c], x_peer)
 
     def x_arrival(c):
-        return moved(c, row, 1 - side, x_send.at[c], x_recv.at[c], x_peer)
+        return moved(c, row, 1 - side, x_send, x_recv.at[c], x_peer)
 
     def f_copy(c, source):
-        return moved(c, source, side, f_send.at[c, source], f_recv.at[c, source], x_peer)
-
-    def f_arrival(c, source):
-        return moved(c, source, 1 - side, f_send.at[c, source], f_recv.at[c, source], x_peer)
+        return moved(c, source, side, f_send.at[source], f_recv.at[c], x_peer)
+
+    def f_arrivals(c):
+        blocks = w_all.at[c, :, 0:last]
+        return remote(blocks, blocks, x_send, f_recv.at[c], x_peer)
+
+    def sent(count, semaphore):
+        blocks = w_all.at[0:count, :, 0]
+        return remote(blocks, blocks, semaphore, x_recv.at[0], x_peer)
 
     def g_copy(c):
-        return moved(c, row, 1 - side, g_send.at[c], f_recv.at[c, row], column(partner))
+        return moved(c, row, 1 - side, g_send, f_recv.at[c], column(partner))
 
     def by_z(c):
-        return lax.rem(c, 2) == 1
+        return c >= chunk_count // 2
 
     def over_x(c, source):
         return jnp.logical_or(jnp.logical_not(by_z(c)), source != partner)
 
     def o_copy(c):
-        return remote(stage.at[c], out.at[y, c], o_send.at[c], o_recv.at[c], y_peer)
+        return remote(stage.at[c], out.at[y, c], o_send, o_recv, y_peer)
 
     def send_own(c):
         for index, (distance, step) in enumerate(hops):
@@ -336,15 +341,16 @@
                 @pl.when(sending)
                 def _():
                     pass_on(c, 1)
-                    x_arrival(c).wait_recv()
-
-                    @pl.when(by_z(c))
-                    def _():
-                        g_copy(c).start()
             elif unit < shard_columns - 1:
                 @pl.when(sending)
                 def _():
                     pass_on(c, unit + 1)
+                    if unit == shard_columns - 2:
+                        x_arrival(c).wait_recv()
+
+                        @pl.when(by_z(c))
+                        def _():
+                            g_copy(c).start()
 
             if unit == shard_columns - 2:
                 @pl.when(c == 1)
@@ -360,8 +366,7 @@
             @pl.when(ready)
             def _():
                 if unit == 0:
-                    for d in range(1, shard_columns):
-                        f_arrival(b, lax.rem(row + d, shard_columns)).wait_recv()
+                    f_arrivals(b).wait_recv()
                     q_copy(b).wait_recv()
                 h = unit % PAIR
                 if unit < PAIR:
@@ -379,39 +384,33 @@
     core_copy.wait_send()
     relay_copy.wait_send()
 
-    def end(c, carry):
-        q_copy(c).wait_send()
-        x_copy(c).wait_send()
-        for index, (distance, step) in enumerate(hops):
-            @pl.when(exists(row + step * distance))
+    direct = chunk_count // 2
+    q_all = q_in.at[1 - y]
+    remote(q_all, q_all, q_send, q_recv.at[0], y_peer).wait_send()
+    sent(chunk_count, x_send).wait_send()
+    sent(direct, g_send).wait_send()
+    for index, (distance, step) in enumerate(hops):
+        @pl.when(exists(row + step * distance))
+        def _():
+            sent(chunk_count, z_send.at[index]).wait_send()
+
+        if distance == 2:
+            @pl.when(jnp.logical_and(exists(row + 2 * step), exists(row - step)))
             def _():
-                z_copy(c, index).wait_send()
-
-            if distance == 2:
-                @pl.when(jnp.logical_and(exists(row + 2 * step), exists(row - step)))
-                def _():
-                    r_copy(c, step).wait_send()
-
-        for d in range(1, shard_columns):
-            other = lax.rem(row + d, shard_columns)
-
-            @pl.when(over_x(c, other))
-            def _():
-                f_copy(c, other).wait_send()
-
-        @pl.when(by_z(c))
+                sent(chunk_count, r_send).wait_send()
+
+    for d in range(1, shard_columns):
+        other = lax.rem(row + d, shard_columns)
+
+        @pl.when(other == partner)
         def _():
-            g_copy(c).wait_send()
-
-        return carry
-
-    lax.fori_loop(0, chunk_count, end, 0)
-
-    def end_out(c, carry):
-        o_copy(c).wait()
-        return carry
-
-    lax.fori_loop(0, chunk_count, end_out, 0)
+            sent(chunk_count - direct, f_send.at[other]).wait_send()
+
+        @pl.when(other != partner)
+        def _():
+            sent(chunk_count, f_send.at[other]).wait_send()
+
+    remote(stage, out.at[y], o_send, o_recv, y_peer).wait()
 
 
 def shared_on_device(
@@ -455,11 +454,11 @@
             vmem((2, pool * page, span), int32),
             vmem((chunks, PAIR, span, nope), bf16),
             dma((6,)), dma, dma, dma, dma, dma, dma, dma, dma,
-            dma((chunks,)), dma((chunks,)),
-            dma((chunks, 4)), dma((chunks, columns)),
-            dma((chunks,)), dma((chunks,)),
-            dma((chunks, columns)), dma((chunks, columns)),
-            dma((chunks,)), dma((chunks,)), dma((chunks,)), dma((chunks,)),
+            dma, dma((chunks,)),
+            dma((4,)), dma((chunks, columns)),
+            dma, dma((chunks,)),
+            dma((columns,)), dma((chunks,)),
+            dma, dma, dma, dma,
         ],
         compiler_params=pltpu.CompilerParams(
             collective_id=0, has_side_effects=True, vmem_limit_bytes=48 * 1024 * 1024

time: 63.7 us -> 60 us (0.942)
  Pallas kernels: 61.2 us -> 57.5 us
    pallas_call x1, Pallas kernels: 61.2 us -> 57.5 us  [shared_on_device(): pl.pallas_call(functools.partial(gather_attend, columns), out_shape=vmem(...]
where the time goes in v2:
time: 60 us; the launch traced here: 59.8 us
  Pallas kernels  57.5 us (96%)
  local copies, waits for them, and re-layouts  1.65 us (3%)
  between operations  0.66 us (1%)
    pallas_call x1, Pallas kernels, shared_on_device(): pl.pallas_call(functools.partial(gather_attend, columns), out_shape=vmem(...  57.5 us
    reshape x1, local copies, waits for them, and re-layouts, shared_on_device(): return jnp.swapaxes(out.reshape(heads, span, nope), 0, 1)[None]  1.65 us

profile of v2, /device:TPU:0, one launch (start us, length us, event | category | flops | bytes accessed | tf_op | source)
XLA Modules:
  0.0 59.8 jit_solution(4999989163758834571)
XLA Ops:
  0.7 57.5 %shard_map.73 = bf16[2,8,2,128,128]{4,3,2,1,0:T(8,128)(2,1)S(1)} custom-call(bf16[2,8,2,192,128]{4,3,2,1,0:T(8,128)(2,1)} %bitcast.14, bf16[4,64,576]{2,1,0:T(8,128)(2,1)} %bitcast.15, bf16[4,4,64]{2,1,0:T(4,128)(2,1)} %bitcast.16, s32[1,8]{1,0:T(1,128)} %table_in.1, bf16[64,32,128]{2,1,0:T(8,128)(2,1)} %wk_in.1, bf16[64,32,128]{2,1,0:T(8,128)(2,1)} %wv_in.1, ...), custom_call_target="tpu_custom_call" | custom-call | tf_op jit(solution)/shard_map/pallas_call | solution.py:435
  58.2 1.6 %copy.10 = bf16[32,128,128]{2,0,1:T(8,128)(2,1)} copy(bf16[32,128,128]{2,1,0:T(8,128)(2,1)S(1)} %bitcast.13) | data formatting | bytes 2097152 | tf_op jit(solution)/shard_map/reshape | solution.py:467

commit v3 on v2

--- a/solution.py
+++ b/solution.py
@@ -133,7 +133,7 @@
     key_count = 2 * page_count * page
     group_count = scales.shape[1]
     group_width = latent_width // group_count
-    scale = 1.0 / math.sqrt(nope + rope)
+    scale = math.log2(math.e) / math.sqrt(nope + rope)
     y, ctx, core = lax.axis_index("groups"), lax.axis_index("ctx"), lax.axis_index("head")
     row, side = ctx // 2, lax.rem(ctx, 2)
     last = shard_columns - 1
@@ -230,8 +230,8 @@
     def over_x(c, source):
         return jnp.logical_or(jnp.logical_not(by_z(c)), source != partner)
 
-    def o_copy(c):
-        return remote(stage.at[c], out.at[y, c], o_send, o_recv, y_peer)
+    def o_copy(c, h):
+        return remote(stage.at[c, h], out.at[y, c, h], o_send, o_recv, y_peer)
 
     def send_own(c):
         for index, (distance, step) in enumerate(hops):
@@ -291,26 +291,24 @@
         offset = offset - lax.broadcasted_iota(jnp.int32, (page, span), 1)
         for request, t_ref in ((y, t_own), (1 - y, t_rx)):
             rot[request] = k_all[request, :, :, :, latent_width:].reshape(key_count, rope)
-            late[request] = jnp.concatenate(
-                [t_ref[p : p + 1] + offset for p in range(slots)], axis=0
-            )
+            behind = jnp.concatenate([t_ref[p : p + 1] + offset for p in range(slots)], axis=0)
+            late[request] = jnp.where(behind <= 0, 0.0, NEGATIVE)
 
     def attend(c, h, request, q_ref):
         latent = k_all[request, :, :, :, :latent_width].reshape(key_count, latent_width)
-        visible = late[request] <= 0
         weight = w_all[c, h].reshape(latent_width, -1)
         up = jnp.dot(latent, weight, preferred_element_type=jnp.float32).astype(jnp.bfloat16)
         keys = jnp.concatenate([up[:, :nope], rot[request]], axis=1)
         scores = jnp.dot(keys, q_ref[c, h], preferred_element_type=jnp.float32)
-        scores = jnp.where(visible, scores * scale, NEGATIVE)
+        scores = scores * scale + late[request]
         top = jnp.max(scores, axis=0, keepdims=True)
-        raw = jnp.where(visible, jnp.exp(scores - top), 0.0)
+        raw = jnp.exp2(scores - top)
         total = jnp.sum(raw, axis=0, keepdims=True)
         summed = lax.dot_general(
             up[:, nope:], raw.astype(jnp.bfloat16), (((0,), (0,)), ((), ())),
             preferred_element_type=jnp.float32,
         )
-        return jnp.transpose(summed / total).astype(jnp.bfloat16)
+        return jnp.transpose(summed * (1.0 / total)).astype(jnp.bfloat16)
 
     def pass_on(c, distance):
         for step in (1, -1):
@@ -341,22 +339,21 @@
                 @pl.when(sending)
                 def _():
                     pass_on(c, 1)
-            elif unit < shard_columns - 1:
+
+            if unit == 1:
                 @pl.when(sending)
                 def _():
-                    pass_on(c, unit + 1)
-                    if unit == shard_columns - 2:
-                        x_arrival(c).wait_recv()
-
-                        @pl.when(by_z(c))
-                        def _():
-                            g_copy(c).start()
-
-            if unit == shard_columns - 2:
-                @pl.when(c == 1)
+                    pass_on(c, 2)
+
+            if unit == 2:
+                @pl.when(sending)
                 def _():
-                    k_copy.wait_recv()
-                    relay_copy.start()
+                    x_arrival(c).wait_recv()
+
+                    @pl.when(by_z(c))
+                    def _():
+                        g_copy(c).start()
+
 
             if unit == 0:
                 @pl.when(c == LAG)
@@ -371,10 +368,18 @@
                 h = unit % PAIR
                 if unit < PAIR:
                     stage[b, h] = attend(b, h, 1 - y, q_rx)
-                    if unit == PAIR - 1:
-                        o_copy(b).start()
+                    o_copy(b, h).start()
                 else:
                     out[y, b, h] = attend(b, h, y, q_own)
+
+        @pl.when(sending)
+        def _():
+            pass_on(c, 3)
+
+        @pl.when(c == LAG - 1)
+        def _():
+            k_copy.wait_recv()
+            relay_copy.start()
 
         return carry
 
@@ -451,7 +456,7 @@
             vmem((latent_rows, half, nope), bf16),
             vmem((chunks, PAIR, shards, latent_rows, 2 * nope), bf16),
             vmem((2, pool * page, rope), bf16),
-            vmem((2, pool * page, span), int32),
+            vmem((2, pool * page, span), jnp.float32),
             vmem((chunks, PAIR, span, nope), bf16),
             dma((6,)), dma, dma, dma, dma, dma, dma, dma, dma,
             dma, dma((chunks,)),

time: 60 us -> 59.3 us (0.988)
  Pallas kernels: 57.5 us -> 56.8 us
    pallas_call x1, Pallas kernels: 57.5 us -> 56.8 us  [shared_on_device(): pl.pallas_call(functools.partial(gather_attend, columns), out_shape=vmem(...]
where the time goes in v3:
time: 59.3 us; the launch traced here: 59.1 us
  Pallas kernels  56.8 us (96%)
  local copies, waits for them, and re-layouts  1.65 us (3%)
  between operations  0.66 us (1%)
    pallas_call x1, Pallas kernels, shared_on_device(): pl.pallas_call(functools.partial(gather_attend, columns), out_shape=vmem(...  56.8 us
    reshape x1, local copies, waits for them, and re-layouts, shared_on_device(): return jnp.swapaxes(out.reshape(heads, span, nope), 0, 1)[None]  1.65 us

profile of v3, /device:TPU:0, one launch (start us, length us, event | category | flops | bytes accessed | tf_op | source)
XLA Modules:
  0.0 59.1 jit_solution(4297339221114392942)
XLA Ops:
  0.7 56.8 %shard_map.73 = bf16[2,8,2,128,128]{4,3,2,1,0:T(8,128)(2,1)S(1)} custom-call(bf16[2,8,2,192,128]{4,3,2,1,0:T(8,128)(2,1)} %bitcast.14, bf16[4,64,576]{2,1,0:T(8,128)(2,1)} %bitcast.15, bf16[4,4,64]{2,1,0:T(4,128)(2,1)} %bitcast.16, s32[1,8]{1,0:T(1,128)} %table_in.1, bf16[64,32,128]{2,1,0:T(8,128)(2,1)} %wk_in.1, bf16[64,32,128]{2,1,0:T(8,128)(2,1)} %wv_in.1, ...), custom_call_target="tpu_custom_call" | custom-call | tf_op jit(solution)/shard_map/pallas_call | solution.py:440
  57.5 1.6 %copy.10 = bf16[32,128,128]{2,0,1:T(8,128)(2,1)} copy(bf16[32,128,128]{2,1,0:T(8,128)(2,1)S(1)} %bitcast.13) | data formatting | bytes 2097152 | tf_op jit(solution)/shard_map/reshape | solution.py:472

commit v4 on v3

--- a/solution.py
+++ b/solution.py
@@ -13,6 +13,8 @@
 PAIR = 2
 LAG = 2
 AHEAD = 3
+INNER = 0
+OUTER = 4
 
 
 def attend_block(
@@ -204,11 +206,15 @@
         source = row + 2 * step
         return moved(c, source, side, r_send, z_recv.at[c, source], column(row - step))
 
+    def two(c, shard, send, recv, peer):
+        blocks = w_all.at[pl.ds(c, 2), :, shard]
+        return remote(blocks, blocks, send, recv, peer)
+
     def x_copy(c):
-        return moved(c, row, side, x_send, x_recv.at[c], x_peer)
+        return two(c, ctx, x_send, x_recv.at[c // 2], x_peer)
 
     def x_arrival(c):
-        return moved(c, row, 1 - side, x_send, x_recv.at[c], x_peer)
+        return two(c, 2 * row + 1 - side, x_send, x_recv.at[c // 2], x_peer)
 
     def f_copy(c, source):
         return moved(c, source, side, f_send.at[source], f_recv.at[c], x_peer)
@@ -224,11 +230,17 @@
     def g_copy(c):
         return moved(c, row, 1 - side, g_send, f_recv.at[c], column(partner))
 
-    def by_z(c):
-        return c >= chunk_count // 2
+    def inner(r):
+        return jnp.logical_and(r > 0, r < last)
+
+    def first_by_z(r):
+        return jnp.where(inner(r), INNER, OUTER)
+
+    def by_z(c, r):
+        return c >= first_by_z(r)
 
     def over_x(c, source):
-        return jnp.logical_or(jnp.logical_not(by_z(c)), source != partner)
+        return jnp.logical_or(jnp.logical_not(by_z(c, row)), source != partner)
 
     def o_copy(c, h):
         return remote(stage.at[c, h], out.at[y, c, h], o_send, o_recv, y_peer)
@@ -239,7 +251,9 @@
             def _():
                 z_copy(c, index).start()
 
-        x_copy(c).start()
+        @pl.when(lax.rem(c, 2) == 0)
+        def _():
+            x_copy(c).start()
 
     loads[0].wait()
     loads[1].wait()
@@ -344,13 +358,11 @@
                 @pl.when(sending)
                 def _():
                     pass_on(c, 2)
-
-            if unit == 2:
-                @pl.when(sending)
-                def _():
-                    x_arrival(c).wait_recv()
-
-                    @pl.when(by_z(c))
+                    @pl.when(lax.rem(c, 2) == 0)
+                    def _():
+                        x_arrival(c).wait_recv()
+
+                    @pl.when(by_z(c, partner))
                     def _():
                         g_copy(c).start()
 
@@ -389,11 +401,14 @@
     core_copy.wait_send()
     relay_copy.wait_send()
 
-    direct = chunk_count // 2
     q_all = q_in.at[1 - y]
     remote(q_all, q_all, q_send, q_recv.at[0], y_peer).wait_send()
     sent(chunk_count, x_send).wait_send()
-    sent(direct, g_send).wait_send()
+    for inside, first in ((True, INNER), (False, OUTER)):
+        @pl.when(inner(partner) == inside)
+        def _():
+            sent(chunk_count - first, g_send).wait_send()
+
     for index, (distance, step) in enumerate(hops):
         @pl.when(exists(row + step * distance))
         def _():
@@ -407,9 +422,11 @@
     for d in range(1, shard_columns):
         other = lax.rem(row + d, shard_columns)
 
-        @pl.when(other == partner)
-        def _():
-            sent(chunk_count - direct, f_send.at[other]).wait_send()
+        for inside, first in ((True, INNER), (False, OUTER)):
+            if first > 0:
+                @pl.when(jnp.logical_and(other == partner, inner(row) == inside))
+                def _():
+                    sent(first, f_send.at[other]).wait_send()
 
         @pl.when(other != partner)
         def _():

time: 59.3 us -> 58 us (0.978)
  Pallas kernels: 56.8 us -> 55.6 us
    pallas_call x1, Pallas kernels: 56.8 us -> 55.6 us  [shared_on_device(): pl.pallas_call(functools.partial(gather_attend, columns), out_shape=vmem(...]
where the time goes in v4:
time: 58 us; the launch traced here: 57.9 us
  Pallas kernels  55.6 us (96%)
  local copies, waits for them, and re-layouts  1.65 us (3%)
  between operations  0.66 us (1%)
    pallas_call x1, Pallas kernels, shared_on_device(): pl.pallas_call(functools.partial(gather_attend, columns), out_shape=vmem(...  55.6 us
    reshape x1, local copies, waits for them, and re-layouts, shared_on_device(): return jnp.swapaxes(out.reshape(heads, span, nope), 0, 1)[None]  1.65 us

profile of v4, /device:TPU:0, one launch (start us, length us, event | category | flops | bytes accessed | tf_op | source)
XLA Modules:
  0.0 57.9 jit_solution(13110516407800008472)
XLA Ops:
  0.7 55.6 %shard_map.73 = bf16[2,8,2,128,128]{4,3,2,1,0:T(8,128)(2,1)S(1)} custom-call(bf16[2,8,2,192,128]{4,3,2,1,0:T(8,128)(2,1)} %bitcast.14, bf16[4,64,576]{2,1,0:T(8,128)(2,1)} %bitcast.15, bf16[4,4,64]{2,1,0:T(4,128)(2,1)} %bitcast.16, s32[1,8]{1,0:T(1,128)} %table_in.1, bf16[64,32,128]{2,1,0:T(8,128)(2,1)} %wk_in.1, bf16[64,32,128]{2,1,0:T(8,128)(2,1)} %wv_in.1, ...), custom_call_target="tpu_custom_call" | custom-call | tf_op jit(solution)/shard_map/pallas_call | solution.py:457
  56.2 1.6 %copy.10 = bf16[32,128,128]{2,0,1:T(8,128)(2,1)} copy(bf16[32,128,128]{2,1,0:T(8,128)(2,1)S(1)} %bitcast.13) | data formatting | bytes 2097152 | tf_op jit(solution)/shard_map/reshape | solution.py:489

commit v5 on v4

--- a/solution.py
+++ b/solution.py
@@ -12,7 +12,7 @@
 MESH = pl.DeviceIdType.MESH
 PAIR = 2
 LAG = 2
-AHEAD = 3
+AHEAD = 4
 INNER = 0
 OUTER = 4
 
@@ -166,10 +166,19 @@
         load.start()
 
     barrier = pltpu.get_barrier_semaphore()
-    peers = [y_peer, core_peer, x_peer]
-    peers += [column(lax.rem(row + d, shard_columns)) for d in range(1, shard_columns)]
-    for peer in peers:
+    hops = [(distance, step) for distance in (1, 2) for step in (1, -1)]
+    arrivals = 3
+    for peer in (y_peer, core_peer, x_peer):
         pl.semaphore_signal(barrier, inc=1, device_id=peer, device_id_type=MESH)
+    for distance, step in hops:
+        here = exists(row + step * distance)
+        arrivals = arrivals + here.astype(jnp.int32)
+
+        @pl.when(here)
+        def _():
+            pl.semaphore_signal(
+                barrier, inc=1, device_id=column(row + step * distance), device_id_type=MESH
+            )
 
     def remote(source, target, send, recv, peer):
         return pltpu.make_async_remote_copy(
@@ -190,8 +199,6 @@
 
     def q_copy(c):
         return remote(q_in.at[1 - y, c], q_rx.at[c], q_send, q_recv.at[c], y_peer)
-
-    hops = [(distance, step) for distance in (1, 2) for step in (1, -1)]
 
     def z_copy(c, index):
         distance, step = hops[index]
@@ -264,7 +271,7 @@
             w_all[c, h, ctx, :, :nope] = keys_by_head[c * PAIR + h]
             w_all[c, h, ctx, :, nope:] = values_by_head[c * PAIR + h]
 
-    pl.semaphore_wait(barrier, len(peers))
+    pl.semaphore_wait(barrier, arrivals)
     for c in range(AHEAD):
         send_own(c)
 
@@ -322,7 +329,7 @@
             up[:, nope:], raw.astype(jnp.bfloat16), (((0,), (0,)), ((), ())),
             preferred_element_type=jnp.float32,
         )
-        return jnp.transpose(summed * (1.0 / total)).astype(jnp.bfloat16)
+        return jnp.transpose((summed * (1.0 / total)).astype(jnp.bfloat16))
 
     def pass_on(c, distance):
         for step in (1, -1):
@@ -341,10 +348,6 @@
                     f_copy(c, source).start()
 
     def advance(c, carry):
-        @pl.when(c + AHEAD < chunk_count)
-        def _():
-            send_own(c + AHEAD)
-
         sending = c < chunk_count
         ready = c >= LAG
         b = jnp.maximum(c - LAG, 0)
@@ -387,6 +390,10 @@
         @pl.when(sending)
         def _():
             pass_on(c, 3)
+
+        @pl.when(c + AHEAD < chunk_count)
+        def _():
+            send_own(c + AHEAD)
 
         @pl.when(c == LAG - 1)
         def _():

time: 58 us -> 58 us (level)
  no operation moved by 1% of the time
where the time goes in v5:
time: 58 us; the launch traced here: 57.8 us
  Pallas kernels  55.5 us (96%)
  local copies, waits for them, and re-layouts  1.65 us (3%)
  between operations  0.66 us (1%)
    pallas_call x1, Pallas kernels, shared_on_device(): pl.pallas_call(functools.partial(gather_attend, columns), out_shape=vmem(...  55.5 us
    reshape x1, local copies, waits for them, and re-layouts, shared_on_device(): return jnp.swapaxes(out.reshape(heads, span, nope), 0, 1)[None]  1.65 us

profile of v5, /device:TPU:0, one launch (start us, length us, event | category | flops | bytes accessed | tf_op | source)
XLA Modules:
  0.0 57.8 jit_solution(4644940921927613447)
XLA Ops:
  0.7 55.5 %shard_map.73 = bf16[2,8,2,128,128]{4,3,2,1,0:T(8,128)(2,1)S(1)} custom-call(bf16[2,8,2,192,128]{4,3,2,1,0:T(8,128)(2,1)} %bitcast.14, bf16[4,64,576]{2,1,0:T(8,128)(2,1)} %bitcast.15, bf16[4,4,64]{2,1,0:T(4,128)(2,1)} %bitcast.16, s32[1,8]{1,0:T(1,128)} %table_in.1, bf16[64,32,128]{2,1,0:T(8,128)(2,1)} %wk_in.1, bf16[64,32,128]{2,1,0:T(8,128)(2,1)} %wv_in.1, ...), custom_call_target="tpu_custom_call" | custom-call | tf_op jit(solution)/shard_map/pallas_call | solution.py:464
  56.2 1.6 %copy.10 = bf16[32,128,128]{2,0,1:T(8,128)(2,1)} copy(bf16[32,128,128]{2,1,0:T(8,128)(2,1)S(1)} %bitcast.13) | data formatting | bytes 2097152 | tf_op jit(solution)/shard_map/reshape | solution.py:496
